TPU v7x, 128 devices: a whole 4x4x4 slice. The times are simulated.
128 devices in a mesh: lat: 32 (over z, y, x_hi), lev: 4 (over x_lo, core).
Axes of the slice: x: 4 (x_hi: 2, x_lo: 2; x = x_hi * 2 + x_lo), y: 4, z: 4, core: 2. Of those that a mesh axis runs over, the one named last changes fastest.
Arguments:
- spec_in: bfloat16 [192, 171, 4, 512], P('lat', None, None, 'lev'), may hold values from -6 to 6
- cotangent: bfloat16 [192, 171, 4, 512], P('lat', None, None, 'lev'), may hold values from -6 to 6
- legendre: bfloat16 [192, 171, 256], P('lat'), may hold values from -0.4375 to 0.4375
- quad_weights: float32 [256], replicated, may hold values from 0.5 to 2
- wave_order: int32 [192], replicated, may hold values from 0 to 191, each once
- norm_gain: float32 [256], replicated, may hold values from 0.5 to 1.5
- weight_in: bfloat16 [256, 512], replicated, may hold values from -0.375 to 0.375
- bias_in: float32 [512], replicated, may hold values from -3 to 3
- weight_mid: bfloat16 [512, 512], replicated, may hold values from -0.25 to 0.25
- bias_mid: float32 [512], replicated, may hold values from -3 to 3
- weight_out: bfloat16 [512, 256], replicated, may hold values from -0.25 to 0.25
Outputs:
- grad_spec: float32 [192, 171, 4, 512], P('lat', None, None, 'lev')
- grad_gain: float32 [256], replicated
- grad_w_in: float32 [256, 512], replicated
- grad_b_in: float32 [512], replicated
- grad_w_mid: float32 [512, 512], replicated
- grad_b_mid: float32 [512], replicated
- grad_w_out: float32 [512, 256], replicated
Inputs may be any that keep to these rules, and one draw needn't show every extreme that they name: `wave_order`: each of 0 to 191 appears once; a slot holding 171 or more is unused.
All inputs are finite; a program needn't handle non-finite values.
Results may differ from a plain program's by a relative error of at most 0.007.
Values may be sent and summed in bfloat16 or wider, within the bound.
A program may use at most 128 MiB of HBM per device.

v0:
```python
import math
import jax
import jax.numpy as jnp
from jax import lax
from jax.sharding import PartitionSpec as P

WAVES = 171
NLAT = 256
NLON = 512
MEMBERS = 4
time_step = 0.5
norm_eps = 1e-06


def in_one_piece(arrays, axis, split_dim, concat_dim, along):
    ends, at = ([], 0)
    for a in arrays[:-1]:
        at += a.shape[along]
        ends.append(at)
    both = jnp.concatenate(arrays, axis=along)
    return tuple(
        jnp.split(
            lax.all_to_all(both, axis, split_axis=split_dim, concat_axis=concat_dim, tiled=True),
            ends,
            axis=along,
        )
    )


def spectral_masks(waves_held, degree_count):
    degree = jnp.arange(degree_count, dtype=jnp.int32)
    living = (waves_held[:, None] <= degree[None, :]) & (waves_held[:, None] < WAVES)
    ratio = (degree * (degree + 1)).astype(jnp.float32) / float(WAVES * (WAVES - 1))
    factor = 1.0 / (1.0 + ratio * ratio)
    shrink = jnp.where(living, factor[None, :], jnp.zeros_like(factor)[None, :])
    return (living, shrink)


def fourier_table(waves_all):
    longitude = jnp.arange(NLON, dtype=jnp.int32)
    phase_steps = waves_all[:, None] * longitude[None, :] % NLON
    angles = phase_steps.astype(jnp.float32) * (2.0 * math.pi / NLON)
    weight_scale = jnp.where(waves_all < WAVES, math.sqrt(2.0 / NLON), 0.0).astype(jnp.float32)[
        :, None
    ]
    return jnp.stack(
        [jnp.cos(angles) * weight_scale, -jnp.sin(angles) * weight_scale], axis=1
    ).astype(jnp.bfloat16)


def contract_rows(left, right):
    return lax.dot_general(
        left, right, (((0,), (0,)), ((), ())), preferred_element_type=jnp.float32
    )


def contract_cols(left, right):
    return lax.dot_general(
        left, right, (((1,), (1,)), ((), ())), preferred_element_type=jnp.float32
    )


def column_grads(
    columns, column_cot, norm_gain, weight_in, bias_in, weight_mid, bias_mid, weight_out
):
    inputs = columns.astype(jnp.float32)
    inverse = lax.rsqrt(jnp.mean(inputs * inputs, axis=1, keepdims=True) + norm_eps)
    normed = (inputs * inverse * norm_gain).astype(jnp.bfloat16)
    pre_one = jnp.dot(normed, weight_in, preferred_element_type=jnp.float32) + bias_in
    sig_one = jax.nn.sigmoid(pre_one)
    act_one = (pre_one * sig_one).astype(jnp.bfloat16)
    pre_two = jnp.dot(act_one, weight_mid, preferred_element_type=jnp.float32) + bias_mid
    sig_two = jax.nn.sigmoid(pre_two)
    act_two = (pre_two * sig_two).astype(jnp.bfloat16)
    gradient_third = contract_rows(act_two, column_cot)
    back_two = contract_cols(column_cot, weight_out)
    delta_two = (back_two * sig_two * (1.0 + pre_two * (1.0 - sig_two))).astype(jnp.bfloat16)
    gradient_second = contract_rows(act_one, delta_two)
    offset_second = jnp.sum(delta_two.astype(jnp.float32), axis=0)
    back_one = contract_cols(delta_two, weight_mid)
    delta_one = (back_one * sig_one * (1.0 + pre_one * (1.0 - sig_one))).astype(jnp.bfloat16)
    gradient_first = contract_rows(normed, delta_one)
    offset_first = jnp.sum(delta_one.astype(jnp.float32), axis=0)
    back_norm = contract_cols(delta_one, weight_in)
    gradient_gain = jnp.sum(back_norm * inputs * inverse, axis=0)
    scaled = back_norm * norm_gain
    grad_columns = inverse * scaled - inputs * inverse * inverse * inverse * jnp.mean(
        scaled * inputs, axis=1, keepdims=True
    )
    return (
        grad_columns.astype(jnp.bfloat16),
        (
            gradient_gain,
            gradient_first,
            offset_first,
            gradient_second,
            offset_second,
            gradient_third,
        ),
    )


def synthesize(wave_table, coeffs):
    shape = coeffs.shape
    split = coeffs.reshape(shape[0], shape[1], shape[2], shape[3] // 2, 2)
    return jnp.einsum(
        "spo,stecp->otec", wave_table, split, preferred_element_type=jnp.float32
    ).astype(jnp.bfloat16)


def analyze(wave_table, values):
    result = jnp.einsum(
        "spo,otec->stecp", wave_table, values, preferred_element_type=jnp.float32
    ).astype(jnp.bfloat16)
    shape = result.shape
    return result.reshape(shape[0], shape[1], shape[2], shape[3] * 2)


def local(
    spec_in,
    cotangent,
    legendre,
    quad_weights,
    wave_order,
    norm_gain,
    weight_in,
    bias_in,
    weight_mid,
    bias_mid,
    weight_out,
):
    slots_here = spec_in.shape[0]
    own_waves = lax.dynamic_slice_in_dim(wave_order, lax.axis_index("lat") * slots_here, slots_here)
    living, shrink = spectral_masks(own_waves, spec_in.shape[1])
    basis_rows = jnp.where(living[:, :, None], legendre, jnp.zeros_like(legendre))
    wave_table = fourier_table(wave_order)
    fourier = jnp.einsum(
        "slt,slek->stek", basis_rows, spec_in, preferred_element_type=jnp.float32
    ).astype(jnp.bfloat16)
    pushed = (time_step * cotangent.astype(jnp.float32) * shrink[:, :, None, None]).astype(
        jnp.bfloat16
    )
    pulled = jnp.einsum("slt,slek->stek", basis_rows, pushed, preferred_element_type=jnp.float32)
    pulled = (quad_weights[None, :, None, None] * pulled).astype(jnp.bfloat16)
    fourier_all, pulled_all = in_one_piece((fourier, pulled), "lat", 1, 0, 2)
    grid_part = synthesize(wave_table, fourier_all)
    cot_part = synthesize(wave_table, pulled_all)
    grid_values, grid_cot = in_one_piece((grid_part, cot_part), "lev", 0, 3, 1)
    grid_shape = grid_values.shape
    grad_rows, grads_local = column_grads(
        grid_values.reshape(-1, grid_shape[3]),
        grid_cot.reshape(-1, grid_shape[3]),
        norm_gain,
        weight_in,
        bias_in,
        weight_mid,
        bias_mid,
        weight_out,
    )
    grad_grid = grad_rows.reshape(grid_shape)
    grad_part = lax.all_to_all(grad_grid, "lev", split_axis=3, concat_axis=0, tiled=True)
    back_fourier = analyze(wave_table, grad_part)
    back_slots = lax.all_to_all(back_fourier, "lat", split_axis=0, concat_axis=1, tiled=True)
    summed = lax.psum(
        (
            grads_local[0],
            grads_local[1],
            grads_local[2],
            grads_local[3],
            grads_local[4],
            grads_local[5],
        ),
        ("lat", "lev"),
    )
    factor = float(MEMBERS * NLAT * NLON) ** (-0.5)
    grads = tuple((piece * factor for piece in summed))
    grad_spec = cotangent.astype(jnp.float32) * shrink[:, :, None, None] + jnp.einsum(
        "slt,stek->slek", basis_rows, back_slots, preferred_element_type=jnp.float32
    )
    return (grad_spec, grads[0], grads[1], grads[2], grads[3], grads[4], grads[5])


def solution(mesh):
    placed = (
        P("lat", None, None, "lev"),
        P("lat", None, None, "lev"),
        P("lat", None, None),
        P(),
        P(),
        P(),
        P(),
        P(),
        P(),
        P(),
        P(),
    )
    return jax.shard_map(
        local,
        mesh=mesh,
        in_specs=placed,
        out_specs=(P("lat", None, None, "lev"), P(), P(), P(), P(), P(), P()),
        check_vma=False,
    )
```

profile of v0, /device:TPU:1, one launch (start us, length us, event | category | flops | bytes accessed | tf_op | source)
XLA Modules:
  0.0 443.2 jit_solution(5164331908292639618)
XLA Ops:
  13.5 3.7 copy.95
  17.2 12.1 %all-to-all-start = ((bf16[6,256,8,128]{3,2,0,1:T(8,128)(2,1)}), bf16[6,256,8,128]{3,2,0,1:T(8,128)(2,1)}, u32[]{:S(2)}, u32[]{:S(2)}) async-start(bf16[6,256,8,128]{3,2,0,1:T(8,128)(2,1)} %copy.95), calls=%async_computation | async-start | bytes 6291456 | tf_op jit(solution)/shard_map/all_to_all | solution.py:23
  31.2 38.7 %all-to-all-done = bf16[6,256,8,128]{3,2,0,1:T(8,128)(2,1)} async-done(((bf16[6,256,8,128]{3,2,0,1:T(8,128)(2,1)}), bf16[6,256,8,128]{3,2,0,1:T(8,128)(2,1)}, u32[]{:S(2)}, u32[]{:S(2)}) %all-to-all-start) | async-done | bytes 3145760 | tf_op jit(solution)/shard_map/all_to_all | solution.py:23
  69.9 2.7 copy.97
  74.9 5.3 %copy.98 = bf16[192,8,4,128]{0,1,3,2:T(8,128)(2,1)} copy(bf16[192,8,4,128]{3,2,1,0:T(4,128)(2,1)} %get-tuple-element.61) | data formatting | bytes 3145728 | tf_op jit(solution)/shard_map/split | solution.py:22
  80.2 4.2 copy.100
  84.4 3.7 bitcast_convert_fusion.1
  92.6 13.8 %copy.102 = bf16[512,16,4,64]{3,2,1,0:T(4,128)(2,1)} copy(bf16[512,16,4,64]{0,3,2,1:T(8,128)(2,1)} %pad_maximum_fusion) | data formatting | bytes 8388608 | tf_op jit(solution)/shard_map/concatenate | solution.py:20
  106.4 9.5 %reshape.301 = bf16[4,2,262144]{2,1,0:T(2,128)(2,1)} reshape(bf16[512,16,4,64]{3,2,1,0:T(4,128)(2,1)} %copy.102) | data formatting | bytes 8388608
  115.9 55.2 %all_to_all.72 = bf16[4,2,262144]{2,1,0:T(2,128)(2,1)} all-to-all(bf16[4,2,262144]{2,1,0:T(2,128)(2,1)} %reshape.301), channel_id=1, replica_groups=mesh['lat'=32,'lev'=4] {'lev'}, dimensions={0} | all-to-all | bytes 8388608 | tf_op jit(solution)/shard_map/all_to_all | solution.py:23
  171.1 9.3 %reshape.302 = bf16[512,16,4,64]{3,2,1,0:T(4,128)(2,1)} reshape(bf16[4,2,262144]{2,1,0:T(2,128)(2,1)} %all_to_all.72) | data formatting | bytes 8388608
  180.4 12.7 %copy.104 = bf16[128,16,4,4,64]{0,4,3,2,1:T(8,128)(2,1)} copy(bf16[128,16,4,4,64]{4,2,1,0,3:T(4,128)(2,1)} %bitcast.65) | data formatting | bytes 8388608 | tf_op jit(solution)/shard_map/all_to_all | solution.py:23
  195.1 4.7 %fusion.44 = (bf16[128,8,4,256]{0,3,2,1:T(8,128)(2,1)S(1)}, f32[128,8,4,256]{0,3,2,1:T(8,128)}) fusion(bf16[128,16,4,256]{0,3,2,1:T(8,128)(2,1)} %bitcast.67), kind=kLoop, calls=%fused_computation.85 | loop fusion | flops 1048576 | bytes 10485760 | tf_op jit(solution)/shard_map/split | solution.py:22
  200.4 2.9 copy.107
  203.2 2.5 reshape.291
  205.8 6.3 %copy.108 = f32[128,8,4,256]{3,2,1,0:T(4,128)} copy(f32[128,8,4,256]{0,3,2,1:T(8,128)} %get-tuple-element.60) | data formatting | bytes 8388608 | tf_op jit(solution)/shard_map/convert_element_type | solution.py:66
  212.1 5.4 %reshape.294 = f32[4096,256]{1,0:T(8,128)} reshape(f32[128,8,4,256]{3,2,1,0:T(4,128)} %copy.108) | data formatting | bytes 8388608 | tf_op jit(solution)/shard_map/convert_element_type | solution.py:66
  217.5 4.9 %multiply_convert_fusion.3 = (bf16[4096,512]{1,0:T(8,128)(2,1)S(1)}, f32[4096,512]{1,0:T(8,128)S(1)}) fusion(f32[512]{0:T(512)S(1)} %copy-done.17, bf16[256,512]{1,0:T(8,128)(2,1)S(1)} %copy-done.10, f32[4096,256]{1,0:T(8,128)} %reshape.294, f32[256]{0:T(256)S(1)} %copy-done.14, f32[4096]{0:T(1024)S(1)} %rsqrt.12), kind=kOutput, calls=%fused_computation.6 | convolution fusion | flops 1089470464 | bytes 17058816 | tf_op jit(solution)/shard_map/dot_general | solution.py:69
  224.9 3.9 convert_reduce_fusion
  228.8 3.3 fusion.47
  232.1 4.4 %convert_reduce_fusion.1 = (f32[512]{0:T(512)S(1)}, bf16[4096,512]{1,0:T(8,128)(2,1)S(1)}) fusion(f32[4096,512]{1,0:T(8,128)S(1)} %get-tuple-element.68, f32[512]{0:T(512)S(1)} %copy-done.17, bf16[4096,512]{1,0:T(8,128)(2,1)S(1)} %get-tuple-element.73, bf16[512,512]{1,0:T(8,128)(2,1)S(1)} %copy-done.9), kind=kOutput, calls=%fused_computation.2 | convolution fusion | flops 2172648960 | bytes 17305600 | tf_op jit(solution)/shard_map/dot_general | solution.py:58
  238.5 3.2 subtract_convert_fusion
  244.3 4.1 copy.109
  248.4 4.7 %all-to-all-start.2 = ((bf16[128,8,4,256]{0,2,1,3:T(4,128)(2,1)}), bf16[128,8,4,256]{0,2,1,3:T(4,128)(2,1)S(1)}, u32[]{:S(2)}, u32[]{:S(2)}) async-start(bf16[128,8,4,256]{0,2,1,3:T(4,128)(2,1)} %copy.109), calls=%async_computation.2 | async-start | bytes 4194304 | tf_op jit(solution)/shard_map/all_to_all | solution.py:161
  253.0 6.9 %fusion.42 = f32[256,512]{1,0:T(8,128)} fusion(bf16[4096,512]{1,0:T(8,128)(2,1)} %copy-done.3, f32[4096,256]{1,0:T(8,128)} %reshape.294, f32[256]{0:T(256)S(1)} %copy-done.14, f32[4096]{0:T(1024)S(1)} %rsqrt.12), kind=kOutput, calls=%fused_computation.83 | convolution fusion | flops 1076887552 | bytes 8930304 | tf_op jit(solution)/shard_map/dot_general | solution.py:52
  259.9 6.6 %fusion = f32[512,256]{1,0:T(8,128)} fusion(bf16[4096,256]{1,0:T(8,128)(2,1)S(1)} %copy-done.8, f32[4096,512]{1,0:T(8,128)} %copy-done.4, f32[512]{0:T(512)S(1)} %copy-done.18), kind=kOutput, calls=%fused_computation.16 | convolution fusion | flops 1086324736 | bytes 11012096 | tf_op jit(solution)/shard_map/dot_general | solution.py:52
  266.6 11.5 %all-to-all-done.2 = bf16[128,8,4,256]{0,2,1,3:T(4,128)(2,1)S(1)} async-done(((bf16[128,8,4,256]{0,2,1,3:T(4,128)(2,1)}), bf16[128,8,4,256]{0,2,1,3:T(4,128)(2,1)S(1)}, u32[]{:S(2)}, u32[]{:S(2)}) %all-to-all-start.2) | async-done | bytes 2097184 | tf_op jit(solution)/shard_map/all_to_all | solution.py:161
  283.3 2.9 convert_bitcast_fusion
  287.4 3.2 copy.113
  290.6 8.0 %all-to-all-start.3 = ((bf16[192,8,4,128]{3,1,2,0:T(8,128)(2,1)}), bf16[192,8,4,128]{3,1,2,0:T(8,128)(2,1)S(1)}, u32[]{:S(2)}, u32[]{:S(2)}) async-start(bf16[192,8,4,128]{3,1,2,0:T(8,128)(2,1)} %copy.113), calls=%async_computation.3 | async-start | bytes 3145728 | tf_op jit(solution)/shard_map/all_to_all | solution.py:163
  298.6 76.6 %all-reduce = (f32[256]{0:T(256)S(1)}, f32[512]{0:T(512)S(1)}, f32[512]{0:T(512)S(1)}) all-reduce(f32[256]{0:T(256)S(1)} %get-tuple-element.49, f32[512]{0:T(512)S(1)} %get-tuple-element.70, f32[512]{0:T(512)S(1)} %get-tuple-element.72), channel_id=1, replica_groups=mesh['lat'=32,'lev'=4] {'lat','lev'}, use_global_device_ids=true, to_apply=%region_3.4 | all-reduce | flops 1280 | bytes 10240 | tf_op jit(solution)/shard_map/psum | solution.py:164
  376.4 49.5 %all-reduce.4.cloned.1.call-done = (f32[256,512]{1,0:T(8,128)}, f32[512,512]{1,0:T(8,128)}, f32[512,256]{1,0:T(8,128)}) async-done(((f32[256,512]{1,0:T(8,128)}, f32[512,512]{1,0:T(8,128)}, f32[512,256]{1,0:T(8,128)}), (f32[256,512]{1,0:T(8,128)}, f32[512,512]{1,0:T(8,128)}, f32[512,256]{1,0:T(8,128)})) %all-reduce.4.cloned.1.call-update) | async-done | bytes 2097168 | tf_op jit(solution)/shard_map/psum | solution.py:164
  (72 shorter events, 42.0 us)
Async XLA Ops:
  7.2 1.6 copy-start
  8.1 2.6 copy-start.12
  17.2 12.1 %copy-start.15 = (s32[192]{0:T(256)S(1)}, s32[192]{0:T(256)}, u32[]{:S(2)}) copy-start(s32[192]{0:T(256)} %param.15) | copy-start | bytes 2308
  17.2 52.7 %all-to-all-start = ((bf16[6,256,8,128]{3,2,0,1:T(8,128)(2,1)}), bf16[6,256,8,128]{3,2,0,1:T(8,128)(2,1)}, u32[]{:S(2)}, u32[]{:S(2)}) async-start(bf16[6,256,8,128]{3,2,0,1:T(8,128)(2,1)} %copy.95), calls=%async_computation | async-start | bytes 6291456 | tf_op jit(solution)/shard_map/all_to_all | solution.py:23
  84.4 3.7 copy-start.6
  205.8 19.1 %copy-start.7 = (bf16[4096,256]{1,0:T(8,128)(2,1)}, bf16[4096,256]{1,0:T(8,128)(2,1)S(1)}, u32[]{:S(2)}) copy-start(bf16[4096,256]{1,0:T(8,128)(2,1)S(1)} %reshape.291) | copy-start | bytes 6291460
  212.1 5.4 %copy-start.10 = (bf16[256,512]{1,0:T(8,128)(2,1)S(1)}, bf16[256,512]{1,0:T(8,128)(2,1)}, u32[]{:S(2)}) copy-start(bf16[256,512]{1,0:T(8,128)(2,1)} %param.17) | copy-start | bytes 786436
  212.1 5.4 %copy-start.14 = (f32[256]{0:T(256)S(1)}, f32[256]{0:T(256)}, u32[]{:S(2)}) copy-start(f32[256]{0:T(256)} %param.16) | copy-start | bytes 3076
  212.1 5.4 %copy-start.17 = (f32[512]{0:T(512)S(1)}, f32[512]{0:T(512)}, u32[]{:S(2)}) copy-start(f32[512]{0:T(512)} %param.18) | copy-start | bytes 6148
  217.5 4.9 %copy-start.9 = (bf16[512,512]{1,0:T(8,128)(2,1)S(1)}, bf16[512,512]{1,0:T(8,128)(2,1)}, u32[]{:S(2)}) copy-start(bf16[512,512]{1,0:T(8,128)(2,1)} %param.19) | copy-start | bytes 1572868
  222.4 2.5 copy-start.16
  222.4 2.5 copy-start.18
  224.9 3.9 copy-start.4
  232.1 4.5 %copy-start.2 = (f32[4096,256]{1,0:T(8,128)S(1)}, f32[4096,256]{1,0:T(8,128)}, u32[]{:S(2)}) copy-start(f32[4096,256]{1,0:T(8,128)} %reshape.294) | copy-start | bytes 12582916
  236.6 1.9 copy-start.3
  248.4 29.7 %all-to-all-start.2 = ((bf16[128,8,4,256]{0,2,1,3:T(4,128)(2,1)}), bf16[128,8,4,256]{0,2,1,3:T(4,128)(2,1)S(1)}, u32[]{:S(2)}, u32[]{:S(2)}) async-start(bf16[128,8,4,256]{0,2,1,3:T(4,128)(2,1)} %copy.109), calls=%async_computation.2 | async-start | bytes 4194304 | tf_op jit(solution)/shard_map/all_to_all | solution.py:161
  253.0 172.9 %all-reduce.4.cloned.1.call-start = ((), (), s32[]{:S(2)}) async-start(), calls=%async_computation.4 | async-start | bytes 4194304 | tf_op jit(solution)/shard_map/psum | solution.py:164
  253.0 6.9 %copy-start.8 = (bf16[4096,256]{1,0:T(8,128)(2,1)S(1)}, bf16[4096,256]{1,0:T(8,128)(2,1)}, u32[]{:S(2)}) copy-start(bf16[4096,256]{1,0:T(8,128)(2,1)} %copy-done.7) | copy-start | bytes 6291460
  290.6 141.4 %copy-start.5 = (bf16[6,171,256]{2,1,0:T(8,128)(2,1)S(1)}, bf16[6,171,256]{2,1,0:T(8,128)(2,1)}, u32[]{:S(2)}) copy-start(bf16[6,171,256]{2,1,0:T(8,128)(2,1)} %param.13) | copy-start | bytes 1575940
  290.6 141.4 %copy-start.11 = (f32[6,171]{1,0:T(8,128)S(1)}, f32[6,171]{1,0:T(8,128)}, u32[]{:S(2)}) copy-start(f32[6,171]{1,0:T(8,128)} %get-tuple-element.63) | copy-start | bytes 12316
  290.6 141.4 %copy-start.13 = (pred[6,171]{1,0:T(8,128)(4,1)S(1)}, pred[6,171]{1,0:T(8,128)(4,1)}, u32[]{:S(2)}) copy-start(pred[6,171]{1,0:T(8,128)(4,1)} %copy-done.12) | copy-start | bytes 3082
  290.6 141.4 %all-to-all-start.3 = ((bf16[192,8,4,128]{3,1,2,0:T(8,128)(2,1)}), bf16[192,8,4,128]{3,1,2,0:T(8,128)(2,1)S(1)}, u32[]{:S(2)}, u32[]{:S(2)}) async-start(bf16[192,8,4,128]{3,1,2,0:T(8,128)(2,1)} %copy.113), calls=%async_computation.3 | async-start | bytes 3145728 | tf_op jit(solution)/shard_map/all_to_all | solution.py:163
  432.0 4.1 copy-start.1
Sparse Core Ops, SparseCore 0:
  266.7 159.1 all-reduce.3
where the time goes:
time: 449 us; the launch traced here: 443 us
  blocking collectives  132 us (29%)
  local copies, waits for them, and re-layouts  99.7 us (22%)
  waiting for transfers between devices  99.7 us (22%)
  matrix products  49.4 us (11%)
  starting transfers between devices  24.8 us (6%)
  other arithmetic  23.3 us (5%)
  between operations  14.6 us (3%)
    psum x1, blocking collectives, local(): lax.psum((grads_local[0], grads_local[1], grads_local[2], grads_local[3],...  76.6 us
    all_to_all x1, blocking collectives, in_one_piece(): lax.all_to_all(both, axis, split_axis=split_dim, concat_axis=concat_dim,...  55.2 us
    psum x1, waiting for transfers between devices, local(): lax.psum((grads_local[0], grads_local[1], grads_local[2], grads_local[3],...  49.5 us
    all_to_all x1, waiting for transfers between devices, in_one_piece(): lax.all_to_all(both, axis, split_axis=split_dim, concat_axis=concat_dim,...  38.7 us
    unnamed x41, local copies, waits for them, and re-layouts  21.1 us
    concatenate x2, local copies, waits for them, and re-layouts, in_one_piece(): both = jnp.concatenate(arrays, axis=along)  17.5 us
    dot_general x3, matrix products, contract_rows(): lax.dot_general(left, right, (((0,), (0,)), ((), ())), preferred_element_...  16.9 us
    all_to_all x2, local copies, waits for them, and re-layouts, in_one_piece(): lax.all_to_all(both, axis, split_axis=split_dim, concat_axis=concat_dim,...  15.5 us
  transfers between devices with their start and end apart: 4, of which 3 were waited for; matrix products, arithmetic and copies ran while one was open for 8% of the time, Pallas kernels for 0%

commit v1 on v0

--- a/solution.py
+++ b/solution.py
@@ -161,17 +161,15 @@
     grad_part = lax.all_to_all(grad_grid, "lev", split_axis=3, concat_axis=0, tiled=True)
     back_fourier = analyze(wave_table, grad_part)
     back_slots = lax.all_to_all(back_fourier, "lat", split_axis=0, concat_axis=1, tiled=True)
-    summed = lax.psum(
-        (
-            grads_local[0],
-            grads_local[1],
-            grads_local[2],
-            grads_local[3],
-            grads_local[4],
-            grads_local[5],
-        ),
-        ("lat", "lev"),
-    )
+    block_here = (
+        grads_local[0],
+        grads_local[1],
+        grads_local[2],
+        grads_local[3],
+        grads_local[4],
+        grads_local[5],
+    )
+    summed = jax.lax.psum(jax.lax.psum(block_here, axis_name="lev"), axis_name="lat")
     factor = float(MEMBERS * NLAT * NLON) ** (-0.5)
     grads = tuple((piece * factor for piece in summed))
     grad_spec = cotangent.astype(jnp.float32) * shrink[:, :, None, None] + jnp.einsum(

time: 449 us -> 708 us (1.58)
  the two profiles are of different devices: /device:TPU:1 before, /device:TPU:4 now
where the time goes in v1:
time: 708 us; the launch traced here: 702 us
  waiting for transfers between devices  282 us (40%)
  blocking collectives  211 us (30%)
  local copies, waits for them, and re-layouts  100 us (14%)
  matrix products  47.7 us (7%)
  other arithmetic  25.1 us (4%)
  starting transfers between devices  21.8 us (3%)
  between operations  14.6 us (2%)
    psum x1, waiting for transfers between devices, local(): jax.lax.psum(jax.lax.psum(block_here, axis_name='lev'), axis_name='lat')  229 us
    psum x1, blocking collectives, local(): jax.lax.psum(jax.lax.psum(block_here, axis_name='lev'), axis_name='lat')  92.7 us
    all_to_all x1, blocking collectives, in_one_piece(): lax.all_to_all(both, axis, split_axis=split_dim, concat_axis=concat_dim,...  54 us
    all_to_all x1, blocking collectives, local(): lax.all_to_all(grad_grid, 'lev', split_axis=3, concat_axis=0, tiled=True)  38.5 us
    all_to_all x1, waiting for transfers between devices, in_one_piece(): lax.all_to_all(both, axis, split_axis=split_dim, concat_axis=concat_dim,...  38.4 us
    psum x1, blocking collectives, local(): jax.lax.psum(block_here, axis_name='lev')  25.4 us
    unnamed x33, local copies, waits for them, and re-layouts  23 us
    concatenate x2, local copies, waits for them, and re-layouts, in_one_piece(): both = jnp.concatenate(arrays, axis=along)  17.5 us
  transfers between devices with their start and end apart: 4, of which 3 were waited for; matrix products, arithmetic and copies ran while one was open for 4% of the time, Pallas kernels for 0%

profile of v1, /device:TPU:4, one launch (start us, length us, event | category | flops | bytes accessed | tf_op | source)
XLA Modules:
  0.0 701.9 jit_solution(9368156778170796093)
XLA Ops:
  13.5 3.7 copy.95
  17.2 11.2 %all-to-all-start = ((bf16[6,256,8,128]{3,2,0,1:T(8,128)(2,1)}), bf16[6,256,8,128]{3,2,0,1:T(8,128)(2,1)}, u32[]{:S(2)}, u32[]{:S(2)}) async-start(bf16[6,256,8,128]{3,2,0,1:T(8,128)(2,1)} %copy.95), calls=%async_computation | async-start | bytes 6291456 | tf_op jit(solution)/shard_map/all_to_all | solution.py:23
  30.9 38.4 %all-to-all-done = bf16[6,256,8,128]{3,2,0,1:T(8,128)(2,1)} async-done(((bf16[6,256,8,128]{3,2,0,1:T(8,128)(2,1)}), bf16[6,256,8,128]{3,2,0,1:T(8,128)(2,1)}, u32[]{:S(2)}, u32[]{:S(2)}) %all-to-all-start) | async-done | bytes 3145760 | tf_op jit(solution)/shard_map/all_to_all | solution.py:23
  74.2 5.3 copy.98
  79.6 4.2 copy.100
  83.8 3.7 bitcast_convert_fusion.1
  91.9 13.8 %copy.102 = bf16[512,16,4,64]{3,2,1,0:T(4,128)(2,1)} copy(bf16[512,16,4,64]{0,3,2,1:T(8,128)(2,1)} %pad_maximum_fusion) | data formatting | bytes 8388608 | tf_op jit(solution)/shard_map/concatenate | solution.py:20
  105.7 9.5 %reshape.301 = bf16[4,2,262144]{2,1,0:T(2,128)(2,1)} reshape(bf16[512,16,4,64]{3,2,1,0:T(4,128)(2,1)} %copy.102) | data formatting | bytes 8388608
  115.2 54.0 %all_to_all.72 = bf16[4,2,262144]{2,1,0:T(2,128)(2,1)} all-to-all(bf16[4,2,262144]{2,1,0:T(2,128)(2,1)} %reshape.301), channel_id=1, replica_groups=mesh['lat'=32,'lev'=4] {'lev'}, dimensions={0} | all-to-all | bytes 8388608 | tf_op jit(solution)/shard_map/all_to_all | solution.py:23
  169.3 9.3 %reshape.302 = bf16[512,16,4,64]{3,2,1,0:T(4,128)(2,1)} reshape(bf16[4,2,262144]{2,1,0:T(2,128)(2,1)} %all_to_all.72) | data formatting | bytes 8388608
  178.5 12.7 %copy.104 = bf16[128,16,4,4,64]{0,4,3,2,1:T(8,128)(2,1)} copy(bf16[128,16,4,4,64]{4,2,1,0,3:T(4,128)(2,1)} %bitcast.65) | data formatting | bytes 8388608 | tf_op jit(solution)/shard_map/all_to_all | solution.py:23
  193.3 4.7 fusion.44
  198.6 2.9 copy.107
  204.0 5.5 copy.108
  209.5 5.3 reshape.294
  214.9 4.9 multiply_convert_fusion.3
  222.2 3.4 fusion
  225.6 3.8 convert_reduce_fusion
  229.5 3.3 fusion.47
  232.8 4.5 convert_reduce_fusion.1
  239.3 3.3 fusion.42
  242.6 6.9 multiply_reduce_fusion
  249.6 5.1 subtract_convert_fusion
  257.2 4.1 copy.109
  261.2 38.5 %all_to_all.73 = bf16[128,8,4,256]{0,2,1,3:T(4,128)(2,1)S(1)} all-to-all(bf16[128,8,4,256]{0,2,1,3:T(4,128)(2,1)} %copy.109), channel_id=1, replica_groups=mesh['lat'=32,'lev'=4] {'lev'}, dimensions={3} | all-to-all | bytes 4194304 | tf_op jit(solution)/shard_map/all_to_all | solution.py:161
  304.8 14.4 %all-reduce.9.cloned.1.call-done = (f32[256,512]{1,0:T(8,128)}, f32[512,512]{1,0:T(8,128)}, f32[512,256]{1,0:T(8,128)}) async-done(((f32[256,512]{1,0:T(8,128)}, f32[512,512]{1,0:T(8,128)}, f32[512,256]{1,0:T(8,128)}), (f32[256,512]{1,0:T(8,128)}, f32[512,512]{1,0:T(8,128)}, f32[512,256]{1,0:T(8,128)})) %all-reduce.9.cloned.1.call-update) | async-done | bytes 2097168 | tf_op jit(solution)/shard_map/psum | solution.py:172
  319.2 2.9 convert_bitcast_fusion
  323.3 3.2 copy.113
  326.5 10.0 %all-to-all-start.3 = ((bf16[192,8,4,128]{3,1,2,0:T(8,128)(2,1)}), bf16[192,8,4,128]{3,1,2,0:T(8,128)(2,1)S(1)}, u32[]{:S(2)}, u32[]{:S(2)}) async-start(bf16[192,8,4,128]{3,1,2,0:T(8,128)(2,1)} %copy.113), calls=%async_computation.3 | async-start | bytes 3145728 | tf_op jit(solution)/shard_map/all_to_all | solution.py:163
  336.5 25.4 %all-reduce.2 = (f32[256]{0:T(256)S(1)}, f32[512]{0:T(512)S(1)}, f32[512]{0:T(512)S(1)}) all-reduce(f32[256]{0:T(256)S(1)} %get-tuple-element.49, f32[512]{0:T(512)S(1)} %get-tuple-element.76, f32[512]{0:T(512)S(1)} %get-tuple-element.78), channel_id=1, replica_groups=mesh['lat'=32,'lev'=4] {'lev'}, use_global_device_ids=true, to_apply=%region_3.4 | all-reduce | flops 1280 | bytes 10240 | tf_op jit(solution)/shard_map/psum | solution.py:172
  361.9 92.7 %all-reduce = (f32[256]{0:T(256)S(1)}, f32[512]{0:T(512)S(1)}, f32[512]{0:T(512)S(1)}) all-reduce(f32[256]{0:T(256)S(1)} %get-tuple-element.57, f32[512]{0:T(512)S(1)} %get-tuple-element.58, f32[512]{0:T(512)S(1)} %get-tuple-element.59), channel_id=1, replica_groups=mesh['lat'=32,'lev'=4] {'lat'}, use_global_device_ids=true, to_apply=%region_4.5 | all-reduce | flops 1280 | bytes 10240 | tf_op jit(solution)/shard_map/psum | solution.py:172
  460.0 228.8 %all-reduce.7.cloned.1.call-done = (f32[256,512]{1,0:T(8,128)}, f32[512,512]{1,0:T(8,128)}, f32[512,256]{1,0:T(8,128)}) async-done(((f32[256,512]{1,0:T(8,128)}, f32[512,512]{1,0:T(8,128)}, f32[512,256]{1,0:T(8,128)}), (f32[256,512]{1,0:T(8,128)}, f32[512,512]{1,0:T(8,128)}, f32[512,256]{1,0:T(8,128)})) %all-reduce.7.cloned.1.call-update) | async-done | bytes 2097168 | tf_op jit(solution)/shard_map/psum | solution.py:172
  (67 shorter events, 47.8 us)
Async XLA Ops:
  7.2 1.6 copy-start
  8.1 2.6 copy-start.8
  17.2 11.8 %copy-start.11 = (s32[192]{0:T(256)S(1)}, s32[192]{0:T(256)}, u32[]{:S(2)}) copy-start(s32[192]{0:T(256)} %param.15) | copy-start | bytes 2308
  17.2 52.1 %all-to-all-start = ((bf16[6,256,8,128]{3,2,0,1:T(8,128)(2,1)}), bf16[6,256,8,128]{3,2,0,1:T(8,128)(2,1)}, u32[]{:S(2)}, u32[]{:S(2)}) async-start(bf16[6,256,8,128]{3,2,0,1:T(8,128)(2,1)} %copy.95), calls=%async_computation | async-start | bytes 6291456 | tf_op jit(solution)/shard_map/all_to_all | solution.py:23
  28.4 290.8 %all-reduce.9.cloned.1.call-start = ((), (), s32[]{:S(2)}) async-start(), calls=%async_computation.5 | async-start | bytes 4194304 | tf_op jit(solution)/shard_map/psum | solution.py:172
  83.8 3.7 copy-start.4
  209.5 5.3 copy-start.6
  209.5 5.3 copy-start.10
  209.5 5.3 copy-start.14
  214.8 4.9 copy-start.5
  219.8 2.4 copy-start.13
  222.2 3.4 copy-start.12
  232.8 6.4 copy-start.2
  237.3 2.0 copy-start.3
  249.5 439.2 %all-reduce.7.cloned.1.call-start = ((), (), s32[]{:S(2)}) async-start(), calls=%async_computation.4 | async-start | bytes 4194304 | tf_op jit(solution)/shard_map/psum | solution.py:172
  323.3 132.4 %copy-start.7 = (f32[6,171]{1,0:T(8,128)S(1)}, f32[6,171]{1,0:T(8,128)}, u32[]{:S(2)}) copy-start(f32[6,171]{1,0:T(8,128)} %get-tuple-element.69) | copy-start | bytes 12316
  323.3 132.4 %copy-start.9 = (pred[6,171]{1,0:T(8,128)(4,1)S(1)}, pred[6,171]{1,0:T(8,128)(4,1)}, u32[]{:S(2)}) copy-start(pred[6,171]{1,0:T(8,128)(4,1)} %copy-done.8) | copy-start | bytes 3082
  326.5 129.2 %all-to-all-start.3 = ((bf16[192,8,4,128]{3,1,2,0:T(8,128)(2,1)}), bf16[192,8,4,128]{3,1,2,0:T(8,128)(2,1)S(1)}, u32[]{:S(2)}, u32[]{:S(2)}) async-start(bf16[192,8,4,128]{3,1,2,0:T(8,128)(2,1)} %copy.113), calls=%async_computation.3 | async-start | bytes 3145728 | tf_op jit(solution)/shard_map/all_to_all | solution.py:163
  455.8 239.0 %copy-start.1 = (bf16[6,171,4,128]{3,2,1,0:T(4,128)(2,1)S(1)}, bf16[6,171,4,128]{3,2,1,0:T(4,128)(2,1)}, u32[]{:S(2)}) copy-start(bf16[6,171,4,128]{3,2,1,0:T(4,128)(2,1)} %param.11) | copy-start | bytes 3151876
Sparse Core Ops, SparseCore 0:
  249.6 69.5 all-reduce.8
  321.9 366.7 all-reduce.6
